TPU v7x, 128 devices: a whole 4x4x4 slice. The times are simulated.
128 devices in a mesh: bank: 4 (over y_lo, core), zero: 32 (over z, y_hi, x).
Axes of the slice: x: 4, y: 4 (y_hi: 2, y_lo: 2; y = y_hi * 2 + y_lo), z: 4, core: 2. Of those that a mesh axis runs over, the one named last changes fastest.
Arguments:
- master_down: float32 [16, 6400, 4096], P('bank', None, 'zero'), may hold values from -0.078125 to 0.078125
- router_weight: float32 [4096, 16], P('zero', 'bank'), may hold values from -0.09375 to 0.09375
- router_gain: float32 [4096], P('zero'), may hold values from 0.25 to 1.75
Outputs:
- final_down: bfloat16 [16, 4096, 6400], P('bank', None, 'zero')
- serve_router: bfloat16 [4096, 16], replicated
All inputs are finite; a program needn't handle non-finite values.
Results may differ from a plain program's by a relative error of at most 0.001.
Values may be sent and summed in bfloat16 or wider, within the bound.
No kernel may reach another device: no remote copies, remote signals or barrier semaphores. Data moves between devices by JAX's collectives and lax.ppermute only.
A program may use at most 128 MiB of HBM per device.

v0:
```python
import jax
import jax.numpy as jnp
from jax import lax
from jax.sharding import PartitionSpec as P


def split_up(value, dim, peers):
    before, after = (value.shape[:dim], value.shape[dim + 1 :])
    return jnp.moveaxis(value.reshape(*before, peers, -1, *after), dim, 0)


def piece_ends(length, count):
    hop = length // count
    if hop >= 8:
        hop -= hop % 8
    return [hop * k for k in range(1, count)]


def laid_out(parts, dim):
    parts = jnp.moveaxis(parts, 0, dim)
    shape = parts.shape
    return parts.reshape(*shape[:dim], shape[dim] * shape[dim + 1], *shape[dim + 2 :])


def several_exchanges(value, axis, pieces, split_dim, concat_dim):
    parts = split_up(value, split_dim, lax.axis_size(axis))
    widest = max(range(1, max(2, parts.ndim - 1)), key=lambda d: parts.shape[d])
    done = []
    for slab in jnp.split(parts, piece_ends(parts.shape[widest], pieces), axis=widest):
        if slab.size:
            done.append(lax.all_to_all(slab, axis, split_axis=0, concat_axis=0, tiled=True))
    return laid_out(jnp.concatenate(done, axis=widest), concat_dim)


def from_everyone(value, axis):
    peers = lax.axis_size(axis)
    return lax.all_to_all(
        jnp.broadcast_to(value[None], (peers, *value.shape)), axis, 0, 0, tiled=True
    )


def gather_directly(value, axis, dim):
    return laid_out(from_everyone(value, axis), dim)


def body(master_down, router_weight, router_gain):
    narrow_down = master_down.astype(jnp.bfloat16)
    final_down = several_exchanges(narrow_down, "zero", 2, 1, 2)
    final_down = jnp.transpose(final_down, (0, 2, 1))
    part_router = (router_weight * router_gain[:, None]).astype(jnp.bfloat16)
    row_router = gather_directly(part_router, "zero", 0)
    serve_router = gather_directly(row_router, "bank", 1)
    return (final_down, serve_router)


def solution(mesh):
    placed = (P("bank", None, "zero"), P("zero", "bank"), P("zero"))
    return jax.shard_map(
        body, mesh=mesh, in_specs=placed, out_specs=(P("bank", None, "zero"), P()), check_vma=False
    )
```

profile of v0, /device:TPU:18, one launch (start us, length us, event | category | flops | bytes accessed | tf_op | source)
XLA Modules:
  0.0 150.7 jit_solution(10382018145954676795)
XLA Ops:
  0.6 0.7 multiply_convert_fusion
  1.3 16.9 %all_to_all.20 = bf16[32,128,4]{1,2,0:T(4,128)(2,1)S(1)} all-to-all(bf16[32,128,4]{1,2,0:T(4,128)(2,1)S(1)} %broadcast_in_dim.6), channel_id=1, replica_groups=mesh['bank'=4,'zero'=32] {'zero'}, dimensions={0} | all-to-all | bytes 65536 | tf_op jit(solution)/shard_map/all_to_all | solution.py:37
  18.3 0.7 broadcast_in_dim.16
  18.9 3.3 %all-to-all-start.3 = ((bf16[4,4096,4]{1,2,0:T(4,128)(2,1)}), bf16[4,4096,4]{1,2,0:T(4,128)(2,1)S(1)}, u32[]{:S(2)}, u32[]{:S(2)}) async-start(bf16[4,4096,4]{1,2,0:T(4,128)(2,1)} %broadcast_in_dim.16), calls=%async_computation.3 | async-start | bytes 262144 | tf_op jit(solution)/shard_map/all_to_all | solution.py:37
  22.3 8.4 %convert_element_type.6 = bf16[4,6400,128]{2,1,0:T(8,128)(2,1)} convert(f32[4,6400,128]{2,1,0:T(8,128)} %param.3) | non-fusion elementwise | flops 3276800 | bytes 19660800 | tf_op jit(solution)/shard_map/convert_element_type | solution.py:47
  30.6 2.2 %split.8 = bf16[32,4,96,128]{3,2,0,1:T(8,128)(2,1)S(1)} slice(bf16[32,4,200,128]{3,2,0,1:T(8,128)(2,1)} %bitcast.15), slice={[0:32], [0:4], [0:96], [0:128]} | slice | bytes 6291456 | tf_op jit(solution)/shard_map/split | solution.py:29
  32.9 2.1 %copy.6 = bf16[32,4,96,128]{3,2,1,0:T(8,128)(2,1)} copy(bf16[32,4,96,128]{3,2,0,1:T(8,128)(2,1)S(1)} %split.8) | data formatting | bytes 6291456 | tf_op jit(solution)/shard_map/split | solution.py:29
  34.9 0.0 all-to-all-done.3
  34.9 7.6 %all-to-all-start = ((bf16[32,4,96,128]{3,2,1,0:T(8,128)(2,1)}), bf16[32,4,96,128]{3,2,1,0:T(8,128)(2,1)S(1)}, u32[]{:S(2)}, u32[]{:S(2)}) async-start(bf16[32,4,96,128]{3,2,1,0:T(8,128)(2,1)} %copy.6), calls=%async_computation | async-start | bytes 6291456 | tf_op jit(solution)/shard_map/all_to_all | solution.py:31
  42.6 2.2 %split.9 = bf16[32,4,104,128]{3,2,0,1:T(8,128)(2,1)S(1)} slice(bf16[32,4,200,128]{3,2,0,1:T(8,128)(2,1)} %bitcast.16), slice={[0:32], [0:4], [96:200], [0:128]} | slice | bytes 6815744 | tf_op jit(solution)/shard_map/split | solution.py:29
  44.8 2.0 %copy.7 = bf16[32,4,104,128]{3,2,1,0:T(8,128)(2,1)} copy(bf16[32,4,104,128]{3,2,0,1:T(8,128)(2,1)S(1)} %split.9) | data formatting | bytes 6815744 | tf_op jit(solution)/shard_map/split | solution.py:29
  46.8 42.9 %all-to-all-done = bf16[32,4,96,128]{3,2,1,0:T(8,128)(2,1)S(1)} async-done(((bf16[32,4,96,128]{3,2,1,0:T(8,128)(2,1)}), bf16[32,4,96,128]{3,2,1,0:T(8,128)(2,1)S(1)}, u32[]{:S(2)}, u32[]{:S(2)}) %all-to-all-start) | async-done | bytes 3145760 | tf_op jit(solution)/shard_map/all_to_all | solution.py:31
  89.7 0.0 copy-start
  89.7 1.6 %copy-done = bf16[32,4,96,128]{3,2,1,0:T(8,128)(2,1)} copy-done((bf16[32,4,96,128]{3,2,1,0:T(8,128)(2,1)}, bf16[32,4,96,128]{3,2,1,0:T(8,128)(2,1)S(1)}, u32[]{:S(2)}) %copy-start) | copy-done | bytes 3145752
  91.3 5.9 %all-to-all-start.1 = ((bf16[32,4,104,128]{3,2,1,0:T(8,128)(2,1)}), bf16[32,4,104,128]{3,2,1,0:T(8,128)(2,1)S(1)}, u32[]{:S(2)}, u32[]{:S(2)}) async-start(bf16[32,4,104,128]{3,2,1,0:T(8,128)(2,1)} %copy.7), calls=%async_computation.1 | async-start | bytes 6815744 | tf_op jit(solution)/shard_map/all_to_all | solution.py:31
  97.2 0.7 reshape.18
  97.9 47.2 %all-to-all-done.1 = bf16[32,4,104,128]{3,2,1,0:T(8,128)(2,1)S(1)} async-done(((bf16[32,4,104,128]{3,2,1,0:T(8,128)(2,1)}), bf16[32,4,104,128]{3,2,1,0:T(8,128)(2,1)S(1)}, u32[]{:S(2)}, u32[]{:S(2)}) %all-to-all-start.1) | async-done | bytes 3407904 | tf_op jit(solution)/shard_map/all_to_all | solution.py:31
  145.1 5.6 %bitcast_bitcast_fusion = bf16[4,4096,200]{1,2,0:T(8,128)(2,1)} fusion(bf16[32,4,104,128]{3,2,1,0:T(8,128)(2,1)S(1)} %all-to-all-done.1, bf16[32,4,96,128]{3,2,1,0:T(8,128)(2,1)} %copy-done), kind=kLoop, calls=%fused_computation | loop fusion | flops 13107200 | bytes 13107200 | tf_op jit(solution)/shard_map/transpose | solution.py:49
  (1 shorter events, 0.0 us)
Async XLA Ops:
  18.9 16.0 %all-to-all-start.3 = ((bf16[4,4096,4]{1,2,0:T(4,128)(2,1)}), bf16[4,4096,4]{1,2,0:T(4,128)(2,1)S(1)}, u32[]{:S(2)}, u32[]{:S(2)}) async-start(bf16[4,4096,4]{1,2,0:T(4,128)(2,1)} %broadcast_in_dim.16), calls=%async_computation.3 | async-start | bytes 262144 | tf_op jit(solution)/shard_map/all_to_all | solution.py:37
  34.9 54.7 %all-to-all-start = ((bf16[32,4,96,128]{3,2,1,0:T(8,128)(2,1)}), bf16[32,4,96,128]{3,2,1,0:T(8,128)(2,1)S(1)}, u32[]{:S(2)}, u32[]{:S(2)}) async-start(bf16[32,4,96,128]{3,2,1,0:T(8,128)(2,1)} %copy.6), calls=%async_computation | async-start | bytes 6291456 | tf_op jit(solution)/shard_map/all_to_all | solution.py:31
  89.7 1.7 %copy-start = (bf16[32,4,96,128]{3,2,1,0:T(8,128)(2,1)}, bf16[32,4,96,128]{3,2,1,0:T(8,128)(2,1)S(1)}, u32[]{:S(2)}) copy-start(bf16[32,4,96,128]{3,2,1,0:T(8,128)(2,1)S(1)} %all-to-all-done) | copy-start | bytes 9437188
  91.3 53.8 %all-to-all-start.1 = ((bf16[32,4,104,128]{3,2,1,0:T(8,128)(2,1)}), bf16[32,4,104,128]{3,2,1,0:T(8,128)(2,1)S(1)}, u32[]{:S(2)}, u32[]{:S(2)}) async-start(bf16[32,4,104,128]{3,2,1,0:T(8,128)(2,1)} %copy.7), calls=%async_computation.1 | async-start | bytes 6815744 | tf_op jit(solution)/shard_map/all_to_all | solution.py:31
where the time goes:
time: 151 us
  waiting for transfers between devices  90.1 us (60%)
  blocking collectives  16.9 us (11%)
  starting transfers between devices  16.8 us (11%)
  other arithmetic  14.7 us (10%)
  local copies, waits for them, and re-layouts  11.6 us (8%)
    all_to_all x2, waiting for transfers between devices, several_exchanges(): lax.all_to_all(slab, axis, split_axis=0, concat_axis=0, tiled=True)  90.1 us
    all_to_all x1, blocking collectives, from_everyone(): lax.all_to_all(jnp.broadcast_to(value[None], (peers, *value.shape)), axis...  16.9 us
    all_to_all x2, starting transfers between devices, several_exchanges(): lax.all_to_all(slab, axis, split_axis=0, concat_axis=0, tiled=True)  13.5 us
    split x4, local copies, waits for them, and re-layouts, several_exchanges(): jnp.split(parts, piece_ends(parts.shape[widest], pieces), axis=widest)  8.54 us
    convert_element_type x1, other arithmetic, body(): narrow_down = master_down.astype(jnp.bfloat16)  8.36 us
    transpose x1, other arithmetic, body(): final_down = jnp.transpose(final_down, (0, 2, 1))  5.64 us
    all_to_all x1, starting transfers between devices, from_everyone(): lax.all_to_all(jnp.broadcast_to(value[None], (peers, *value.shape)), axis...  3.33 us
  transfers between devices with their start and end apart: 3, of which 2 were waited for; matrix products, arithmetic and copies ran while one was open for 12% of the time, Pallas kernels for 0%

commit v1 on v0

v1 whole, which is shorter than its diff:
```python
import functools

import jax
import jax.numpy as jnp
from jax import lax
from jax.experimental import pallas as pl
from jax.experimental.pallas import tpu as pltpu
from jax.sharding import PartitionSpec as P

CHUNKS = ((0, 1), (1, 4))
Z, Y, X = 4, 2, 4
PEERS = Z * Y * X
LISTED = [z * Y * X + y * X + x for x in range(X) for y in range(Y) for z in range(Z)]
BANKS = 4


def narrow_kernel(first, count, rows, slots, down, *rest):
    router, out, wide, slim, come, go, sem = rest if len(rest) == 7 else (None, *rest)
    lump = Y * X * rows
    steps = [(e, z) for e in range(count) for z in range(Z)]

    def fetch(k):
        e, z = steps[k]
        return pltpu.make_async_copy(
            down.at[first + e, pl.ds(z * lump, lump)], wide.at[k % slots], come.at[k % slots]
        )

    def put(k):
        e, z = steps[k]
        return pltpu.make_async_copy(
            slim.at[k % slots], out.at[:, z, pl.ds(e * rows, rows)], go.at[k % slots]
        )

    for k in range(min(slots, len(steps))):
        fetch(k).start()
    if router is not None:
        tail = router.shape[0]
        spread = [
            pltpu.make_async_copy(router, out.at[n, z, pl.ds(count * rows, tail)], sem)
            for n in range(X * Y)
            for z in range(Z)
        ]
        for c in spread:
            c.start()
    for k in range(len(steps)):
        if k >= slots:
            put(k - slots).wait()
        fetch(k).wait()
        for y in range(Y):
            for x in range(X):
                piece = wide[k % slots, pl.ds((y * X + x) * rows, rows)]
                slim[k % slots, x * Y + y] = piece.astype(jnp.bfloat16)
        put(k).start()
        if k + slots < len(steps):
            fetch(k + slots).start()
    for k in range(max(0, len(steps) - slots), len(steps)):
        put(k).wait()
    if router is not None:
        for c in spread:
            c.wait()


def narrow(down, first, last, router=None):
    count, rows = last - first, down.shape[1] // PEERS
    tail = 0 if router is None else router.shape[0]
    slots = 3
    down = pltpu.with_memory_space_constraint(down, pltpu.HBM)
    given = (down,) if router is None else (down, router)
    hbm = pl.BlockSpec(memory_space=pltpu.HBM)
    out = pl.pallas_call(
        functools.partial(narrow_kernel, first, count, rows, slots),
        out_shape=pltpu.HBM((X * Y, Z, count * rows + tail, 128), jnp.bfloat16),
        in_specs=[hbm] + [pl.BlockSpec(memory_space=pltpu.VMEM)] * (len(given) - 1),
        out_specs=hbm,
        scratch_shapes=[
            pltpu.VMEM((slots, Y * X * rows, 128), jnp.float32),
            pltpu.VMEM((slots, X * Y, rows, 128), jnp.bfloat16),
            pltpu.SemaphoreType.DMA((slots,)),
            pltpu.SemaphoreType.DMA((slots,)),
            pltpu.SemaphoreType.DMA,
        ],
        compiler_params=pltpu.CompilerParams(vmem_limit_bytes=8 << 20),
        cost_estimate=pl.CostEstimate(
            flops=count * PEERS * rows * 128 * 40,
            bytes_accessed=count * PEERS * rows * 128 * 6,
            transcendentals=0,
        ),
    )(*given)
    return out.reshape(PEERS, count * rows + tail, 128)


def place_kernel(first, count, rows, tail, aliased, got, *rest):
    rest = rest[1:] if aliased else rest
    final, serve, sem = rest if tail else (rest[0], None, rest[1])
    copies = []
    for at, p in enumerate(LISTED):
        columns = pl.ds(p * 128, 128)
        for e in range(count):
            copies.append((got.at[at, pl.ds(e * rows, rows)], final.at[first + e, :, columns]))
        if tail:
            copies.append((got.at[at, pl.ds(count * rows, tail)], serve.at[:, columns]))
    copies = [pltpu.make_async_copy(a, b, sem) for a, b in copies]
    for c in copies:
        c.start()
    for c in copies:
        c.wait()


def place(got, first, last, experts, rows, tail, final=None):
    count = last - first
    anywhere = pl.BlockSpec(memory_space=pltpu.HBM)
    shapes = [pltpu.HBM((experts, rows, PEERS * 128), jnp.bfloat16)]
    if tail:
        shapes.append(pltpu.HBM((tail, PEERS * 128), jnp.bfloat16))
    got = pltpu.with_memory_space_constraint(got, pltpu.VMEM)
    given = (got,) if final is None else (got, final)
    return pl.pallas_call(
        functools.partial(place_kernel, first, count, rows, tail, final is not None),
        out_shape=shapes,
        in_specs=[pl.BlockSpec(memory_space=pltpu.VMEM)] + [anywhere] * (len(given) - 1),
        out_specs=[anywhere] * len(shapes),
        scratch_shapes=[pltpu.SemaphoreType.DMA],
        input_output_aliases={} if final is None else {1: 0},
        compiler_params=pltpu.CompilerParams(vmem_limit_bytes=8 << 20),
        cost_estimate=pl.CostEstimate(
            flops=count * PEERS * rows * 128 * 20, bytes_accessed=count * PEERS * rows * 128 * 4, transcendentals=0
        ),
    )(*given)


def all_banks(part):
    me = lax.axis_index("bank")
    by_step = [part] + [
        lax.ppermute(part, "bank", [(b, b ^ k) for b in range(BANKS)]) for k in range(1, BANKS)
    ]
    blocks = []
    for g in range(BANKS):
        block = by_step[g]
        for b in range(1, BANKS):
            block = jnp.where(me == b, by_step[g ^ b], block)
        blocks.append(block)
    return jnp.concatenate(blocks, axis=0)


def exchange(sent):
    return lax.all_to_all(sent, "zero", 0, 0, axis_index_groups=[LISTED], tiled=True)


def body(master_down, router_weight, router_gain):
    experts, rows = master_down.shape[0], master_down.shape[1] // PEERS
    part = (router_weight.T * router_gain[None, :]).astype(jnp.bfloat16)
    router = all_banks(part)
    got = []
    for k, (first, last) in enumerate(CHUNKS):
        with_router = router if k == len(CHUNKS) - 1 else None
        got.append(exchange(narrow(master_down, first, last, with_router)))
    final = None
    for k, (first, last) in enumerate(CHUNKS):
        tail = router.shape[0] if k == len(CHUNKS) - 1 else 0
        final, *serve = place(got[k], first, last, experts, rows, tail, final)
    return jnp.transpose(final, (0, 2, 1)), serve[0].T


def solution(mesh):
    placed = (P("bank", None, "zero"), P("zero", "bank"), P("zero"))
    return jax.shard_map(
        body, mesh=mesh, in_specs=placed, out_specs=(P("bank", None, "zero"), P()), check_vma=False
    )
```

time: 151 us -> 129 us (0.85)
  the two profiles are of different devices: /device:TPU:18 before, /device:TPU:94 now
where the time goes in v1:
time: 129 us; the launch traced here: 128 us
  waiting for transfers between devices  81.8 us (63%)
  starting transfers between devices  28.5 us (22%)
  Pallas kernels  17.2 us (13%)
    all_to_all x2, waiting for transfers between devices, exchange(): lax.all_to_all(sent, 'zero', 0, 0, axis_index_groups=[LISTED], tiled=True)  73 us
    all_to_all x2, starting transfers between devices, exchange(): lax.all_to_all(sent, 'zero', 0, 0, axis_index_groups=[LISTED], tiled=True)  26.5 us
    pallas_call x2, Pallas kernels, narrow(): pl.pallas_call(functools.partial(narrow_kernel, first, count, rows, slots...  11.3 us
    ppermute x3, waiting for transfers between devices, all_banks(): lax.ppermute(part, 'bank', [(b, b ^ k) for b in range(BANKS)])  8.79 us
    pallas_call x2, Pallas kernels, place(): pl.pallas_call(functools.partial(place_kernel, first, count, rows, tail,...  5.9 us
  transfers between devices with their start and end apart: 5, of which 3 were waited for; matrix products, arithmetic and copies ran while one was open for 0% of the time, Pallas kernels for 7%

profile of v1, /device:TPU:94, one launch (start us, length us, event | category | flops | bytes accessed | tf_op | source)
XLA Modules:
  0.0 128.3 jit_solution(2612415766622752534)
XLA Ops:
  0.6 0.0 copy-start.1
  0.6 0.0 copy-start
  0.6 3.7 %shard_map.51 = bf16[8,4,200,128]{3,2,1,0:T(8,128)(2,1)} custom-call(f32[4,6400,128]{2,1,0:T(8,128)} %down.3), custom_call_target="tpu_custom_call" | custom-call | flops 32768000 | bytes 4915200 | tf_op jit(solution)/shard_map/pallas_call | solution.py:70
  4.4 10.0 %all-to-all-start.1 = ((bf16[32,200,128]{2,1,0:T(8,128)(2,1)}), bf16[32,200,128]{2,1,0:T(8,128)(2,1)S(1)}, u32[]{:S(2)}, u32[]{:S(2)}) async-start(bf16[32,200,128]{2,1,0:T(8,128)(2,1)} %bitcast.10), calls=%async_computation.1 | async-start | bytes 3276800 | tf_op jit(solution)/shard_map/all_to_all | solution.py:146
  14.4 0.0 copy-done.1
  14.4 0.0 copy-done
  14.4 0.1 collective-permute-start.2
  14.5 0.8 collective-permute-start.1
  15.3 1.0 collective-permute-start
  16.3 0.0 collective-permute-done.2
  16.3 8.8 %collective-permute-done.1 = bf16[4,128]{1,0:T(4,128)(2,1)S(1)} collective-permute-done((bf16[4,128]{1,0:T(4,128)(2,1)S(1)}, bf16[4,128]{1,0:T(4,128)(2,1)S(1)}, u32[]{:S(2)}, u32[]{:S(2)}) %collective-permute-start.1) | collective-permute-done | bytes 1056 | tf_op jit(solution)/shard_map/ppermute | solution.py:134
  25.1 0.0 collective-permute-done
  25.2 7.6 %shard_map.50 = bf16[8,4,616,128]{3,2,1,0:T(8,128)(2,1)} custom-call(f32[4,6400,128]{2,1,0:T(8,128)} %down.3, bf16[16,128]{1,0:T(8,128)(2,1)S(1)} %pad_maximum_fusion.rest_0_), custom_call_target="tpu_custom_call" | custom-call | flops 98304000 | bytes 14745600 | tf_op jit(solution)/shard_map/pallas_call | solution.py:70
  32.8 0.8 all-to-all-done.1.got
  33.6 16.5 %all-to-all-start = ((bf16[32,616,128]{2,1,0:T(8,128)(2,1)}), bf16[32,616,128]{2,1,0:T(8,128)(2,1)}, u32[]{:S(2)}, u32[]{:S(2)}) async-start(bf16[32,616,128]{2,1,0:T(8,128)(2,1)} %bitcast.9), calls=%async_computation | async-start | bytes 10092544 | tf_op jit(solution)/shard_map/all_to_all | solution.py:146
  50.2 1.2 shard_map.52.rest_0_
  51.3 72.2 %all-to-all-done.got = bf16[32,616,128]{2,1,0:T(8,128)(2,1)} async-done(((bf16[32,616,128]{2,1,0:T(8,128)(2,1)}), bf16[32,616,128]{2,1,0:T(8,128)(2,1)}, u32[]{:S(2)}, u32[]{:S(2)}) %all-to-all-start) | async-done | bytes 5046304 | tf_op jit(solution)/shard_map/all_to_all | solution.py:146
  123.5 4.7 %shard_map.53 = (bf16[4,200,4096]{2,1,0:T(8,128)(2,1)}, bf16[16,4096]{1,0:T(8,128)(2,1)}) custom-call(bf16[32,616,128]{2,1,0:T(8,128)(2,1)} %all-to-all-done.got, bf16[4,200,4096]{2,1,0:T(8,128)(2,1)} %shard_map.52.rest_0_), custom_call_target="tpu_custom_call", output_to_operand_aliasing={{0}: (1, {})} | custom-call | flops 49152000 | bytes 9830400 | tf_op jit(solution)/shard_map/pallas_call | solution.py:117
  (3 shorter events, 0.0 us)
Async XLA Ops:
  0.6 13.7 %copy-start.1 = (f32[128]{0:T(128)S(1)}, f32[128]{0:T(128)}, u32[]{:S(2)}) copy-start(f32[128]{0:T(128)} %param.5) | copy-start | bytes 1540
  0.6 13.7 %copy-start = (f32[128,4]{0,1:T(4,128)S(1)}, f32[128,4]{0,1:T(4,128)}, u32[]{:S(2)}) copy-start(f32[128,4]{0,1:T(4,128)} %param.4) | copy-start | bytes 6148
  4.4 29.3 %all-to-all-start.1 = ((bf16[32,200,128]{2,1,0:T(8,128)(2,1)}), bf16[32,200,128]{2,1,0:T(8,128)(2,1)S(1)}, u32[]{:S(2)}, u32[]{:S(2)}) async-start(bf16[32,200,128]{2,1,0:T(8,128)(2,1)} %bitcast.10), calls=%async_computation.1 | async-start | bytes 3276800 | tf_op jit(solution)/shard_map/all_to_all | solution.py:146
  14.4 1.9 %collective-permute-start.2 = (bf16[4,128]{1,0:T(4,128)(2,1)S(1)}, bf16[4,128]{1,0:T(4,128)(2,1)S(1)}, u32[]{:S(2)}, u32[]{:S(2)}) collective-permute-start(bf16[4,128]{1,0:T(4,128)(2,1)S(1)} %fusion), channel_id=1, source_target_pairs={{0,32},{32,0},{64,96},{96,64},{1,33},{33,1},{65,97},{97,65},{2,34}... | collective-permute-start | bytes 3080 | tf_op jit(solution)/shard_map/ppermute | solution.py:134
  14.5 10.6 %collective-permute-start.1 = (bf16[4,128]{1,0:T(4,128)(2,1)S(1)}, bf16[4,128]{1,0:T(4,128)(2,1)S(1)}, u32[]{:S(2)}, u32[]{:S(2)}) collective-permute-start(bf16[4,128]{1,0:T(4,128)(2,1)S(1)} %fusion), channel_id=1, source_target_pairs={{0,64},{32,96},{64,0},{96,32},{1,65},{33,97},{65,1},{97,33},{2,66}... | collective-permute-start | bytes 3080 | tf_op jit(solution)/shard_map/ppermute | solution.py:134
  15.3 9.8 %collective-permute-start = (bf16[4,128]{1,0:T(4,128)(2,1)S(1)}, bf16[4,128]{1,0:T(4,128)(2,1)S(1)}, u32[]{:S(2)}, u32[]{:S(2)}) collective-permute-start(bf16[4,128]{1,0:T(4,128)(2,1)S(1)} %fusion), channel_id=1, source_target_pairs={{0,96},{32,64},{64,32},{96,0},{1,97},{33,65},{65,33},{97,1},{2,98}... | collective-permute-start | bytes 3080 | tf_op jit(solution)/shard_map/ppermute | solution.py:134
  33.6 89.9 %all-to-all-start = ((bf16[32,616,128]{2,1,0:T(8,128)(2,1)}), bf16[32,616,128]{2,1,0:T(8,128)(2,1)}, u32[]{:S(2)}, u32[]{:S(2)}) async-start(bf16[32,616,128]{2,1,0:T(8,128)(2,1)} %bitcast.9), calls=%async_computation | async-start | bytes 10092544 | tf_op jit(solution)/shard_map/all_to_all | solution.py:146

commit v2 on v0

v2 whole, which is shorter than its diff:
```python
import functools

import jax
import jax.numpy as jnp
from jax import lax
from jax.experimental import pallas as pl
from jax.experimental.pallas import tpu as pltpu
from jax.sharding import PartitionSpec as P

Z, Y, X = 4, 2, 4
PEERS = Z * Y * X
LISTED = [z * Y * X + y * X + x for z in range(Z) for x in range(X) for y in range(Y)]
BANKS = 4
LANES = 128
HBM = pl.BlockSpec(memory_space=pltpu.HBM)
VMEM = pl.BlockSpec(memory_space=pltpu.VMEM)


def narrow_kernel(experts, rows, down, out, wide, slim, come, go):
    lump = Y * X * rows
    steps = [(e, z) for e in range(experts) for z in range(Z)]

    def fetch(k):
        e, z = steps[k]
        return pltpu.make_async_copy(
            down.at[e, pl.ds(z * lump, lump)], wide.at[k], come.at[k]
        )

    def put(k):
        e, z = steps[k]
        return pltpu.make_async_copy(
            slim.at[k], out.at[z, :, pl.ds(e * rows, rows)], go.at[k]
        )

    for k in range(len(steps)):
        fetch(k).start()
    for k in range(len(steps)):
        fetch(k).wait()
        for y in range(Y):
            for x in range(X):
                piece = wide[k, pl.ds((y * X + x) * rows, rows)]
                slim[k, x * Y + y] = piece.astype(jnp.bfloat16)
        put(k).start()
    for k in range(len(steps)):
        put(k).wait()


def narrow(down, tail):
    experts, rows = down.shape[0], down.shape[1] // PEERS
    steps = experts * Z
    return pl.pallas_call(
        functools.partial(narrow_kernel, experts, rows),
        out_shape=pltpu.HBM((Z, X * Y, experts * rows + tail, LANES), jnp.bfloat16),
        in_specs=[HBM],
        out_specs=HBM,
        scratch_shapes=[
            pltpu.VMEM((steps, Y * X * rows, LANES), jnp.float32),
            pltpu.VMEM((steps, X * Y, rows, LANES), jnp.bfloat16),
            pltpu.SemaphoreType.DMA((steps,)),
            pltpu.SemaphoreType.DMA((steps,)),
        ],
        compiler_params=pltpu.CompilerParams(vmem_limit_bytes=24 << 20),
        cost_estimate=pl.CostEstimate(
            flops=down.size * 40, bytes_accessed=down.size * 6, transcendentals=0
        ),
    )(pltpu.with_memory_space_constraint(down, pltpu.HBM))


def tuck_kernel(start, router, _, out, sem):
    copies = [
        pltpu.make_async_copy(router, out.at[z, n, pl.ds(start, router.shape[0])], sem)
        for z in range(Z)
        for n in range(X * Y)
    ]
    for c in copies:
        c.start()
    for c in copies:
        c.wait()


def tuck(router, sent):
    return pl.pallas_call(
        functools.partial(tuck_kernel, sent.shape[2] - router.shape[0]),
        out_shape=pltpu.HBM(sent.shape, sent.dtype),
        in_specs=[VMEM, HBM],
        out_specs=HBM,
        scratch_shapes=[pltpu.SemaphoreType.DMA],
        input_output_aliases={1: 0},
        compiler_params=pltpu.CompilerParams(vmem_limit_bytes=2 << 20),
    )(router, sent)


def place_kernel(experts, rows, got, final, serve, sem):
    copies = []
    for at, p in enumerate(LISTED):
        columns = pl.ds(p * LANES, LANES)
        for e in range(experts):
            copies.append((got.at[at, pl.ds(e * rows, rows)], final.at[e, :, columns]))
        copies.append((got.at[at, pl.ds(experts * rows, serve.shape[0])], serve.at[:, columns]))
    copies = [pltpu.make_async_copy(a, b, sem) for a, b in copies]
    for c in copies:
        c.start()
    for c in copies:
        c.wait()


def place(got, experts, rows, tail):
    return pl.pallas_call(
        functools.partial(place_kernel, experts, rows),
        out_shape=[
            pltpu.HBM((experts, rows, PEERS * LANES), jnp.bfloat16),
            pltpu.HBM((tail, PEERS * LANES), jnp.bfloat16),
        ],
        in_specs=[VMEM],
        out_specs=[HBM, HBM],
        scratch_shapes=[pltpu.SemaphoreType.DMA],
        compiler_params=pltpu.CompilerParams(vmem_limit_bytes=8 << 20),
    )(got)


def all_banks(part):
    me = lax.axis_index("bank")
    by_step = [part] + [
        lax.ppermute(part, "bank", [(b, b ^ k) for b in range(BANKS)]) for k in range(1, BANKS)
    ]
    blocks = []
    for g in range(BANKS):
        block = by_step[g]
        for b in range(1, BANKS):
            block = jnp.where(me == b, by_step[g ^ b], block)
        blocks.append(block)
    return jnp.concatenate(blocks, axis=0)


def body(master_down, router_weight, router_gain):
    experts, rows = master_down.shape[0], master_down.shape[1] // PEERS
    part = (router_weight.T * router_gain[None, :]).astype(jnp.bfloat16)
    router = all_banks(part)
    sent = tuck(router, narrow(master_down, router.shape[0]))
    sent = sent.reshape(PEERS, *sent.shape[2:])
    got = lax.all_to_all(sent, "zero", 0, 0, axis_index_groups=[LISTED], tiled=True)
    final, serve = place(got, experts, rows, router.shape[0])
    return jnp.transpose(final, (0, 2, 1)), serve.T


def solution(mesh):
    placed = (P("bank", None, "zero"), P("zero", "bank"), P("zero"))
    return jax.shard_map(
        body, mesh=mesh, in_specs=placed, out_specs=(P("bank", None, "zero"), P()), check_vma=False
    )
```

time: 151 us -> 106 us (0.70)
  the two profiles are of different devices: /device:TPU:18 before, /device:TPU:0 now
where the time goes in v2:
time: 106 us
  blocking collectives  91.2 us (86%)
  Pallas kernels  11.2 us (11%)
  starting transfers between devices  1.85 us (2%)
    all_to_all x1, blocking collectives, body(): lax.all_to_all(sent, 'zero', 0, 0, axis_index_groups=[LISTED], tiled=True)  91.2 us
    pallas_call x1, Pallas kernels, narrow(): pl.pallas_call(functools.partial(narrow_kernel, experts, rows), out_shape...  7.66 us
    pallas_call x1, Pallas kernels, place(): pl.pallas_call(functools.partial(place_kernel, experts, rows), out_shape=...  2.81 us
  transfers between devices with their start and end apart: 3, of which 0 were waited for; matrix products, arithmetic and copies ran while one was open for 0% of the time, Pallas kernels for 7%

profile of v2, /device:TPU:0, one launch (start us, length us, event | category | flops | bytes accessed | tf_op | source)
XLA Modules:
  0.0 105.7 jit_solution(10201020318187322965)
XLA Ops:
  0.6 0.7 fusion
  1.3 0.0 copy-start
  1.3 0.0 copy-start.1
  1.3 0.0 collective-permute-start.2
  1.3 1.8 %collective-permute-start.1 = (bf16[4,128]{1,0:T(4,128)(2,1)S(1)}, bf16[4,128]{1,0:T(4,128)(2,1)S(1)}, u32[]{:S(2)}, u32[]{:S(2)}) collective-permute-start(bf16[4,128]{1,0:T(4,128)(2,1)S(1)} %fusion), channel_id=1, source_target_pairs={{0,64},{32,96},{64,0},{96,32},{1,65},{33,97},{65,1},{97,33},{2,66}... | collective-permute-start | bytes 3080 | tf_op jit(solution)/shard_map/ppermute | solution.py:124
  3.1 0.1 collective-permute-start
  3.2 7.7 %shard_map.50._ = bf16[4,8,816,128]{3,2,1,0:T(8,128)(2,1)} custom-call(f32[4,6400,128]{2,1,0:T(8,128)} %down.1), custom_call_target="tpu_custom_call" | custom-call | flops 131072000 | bytes 19660800 | tf_op jit(solution)/shard_map/pallas_call | solution.py:51
  10.9 0.0 collective-permute-done.2
  10.9 0.0 collective-permute-done.1
  10.9 0.0 collective-permute-done
  10.9 0.0 copy-done
  10.9 0.0 copy-done.1
  10.9 0.7 shard_map.51
  11.7 91.2 %all_to_all.5.got = bf16[32,816,128]{2,1,0:T(8,128)(2,1)S(1)} all-to-all(bf16[32,816,128]{2,1,0:T(8,128)(2,1)} %bitcast.7), channel_id=1, replica_groups={{0,4,1,5,2,6,3,7,8,12,9,13,10,14,11,15,16,20,17,21,18,22,19,23,24,28,25..., dimensions={0} | all-to-all | bytes 13369344 | tf_op jit(solution)/shard_map/all_to_all | solution.py:141
  102.9 2.8 %shard_map.52 = (bf16[4,200,4096]{2,1,0:T(8,128)(2,1)}, bf16[16,4096]{1,0:T(8,128)(2,1)}) custom-call(bf16[32,816,128]{2,1,0:T(8,128)(2,1)S(1)} %all_to_all.5.got), custom_call_target="tpu_custom_call" | custom-call | tf_op jit(solution)/shard_map/pallas_call | solution.py:108
  (2 shorter events, 0.0 us)
Async XLA Ops:
  1.3 9.6 %copy-start = (f32[128,4]{0,1:T(4,128)S(1)}, f32[128,4]{0,1:T(4,128)}, u32[]{:S(2)}) copy-start(f32[128,4]{0,1:T(4,128)} %param.4) | copy-start | bytes 6148
  1.3 9.6 %copy-start.1 = (f32[128]{0:T(128)S(1)}, f32[128]{0:T(128)}, u32[]{:S(2)}) copy-start(f32[128]{0:T(128)} %param.5) | copy-start | bytes 1540
  1.3 9.5 %collective-permute-start.2 = (bf16[4,128]{1,0:T(4,128)(2,1)S(1)}, bf16[4,128]{1,0:T(4,128)(2,1)S(1)}, u32[]{:S(2)}, u32[]{:S(2)}) collective-permute-start(bf16[4,128]{1,0:T(4,128)(2,1)S(1)} %fusion), channel_id=1, source_target_pairs={{0,32},{32,0},{64,96},{96,64},{1,33},{33,1},{65,97},{97,65},{2,34}... | collective-permute-start | bytes 3080 | tf_op jit(solution)/shard_map/ppermute | solution.py:124
  1.3 9.5 %collective-permute-start.1 = (bf16[4,128]{1,0:T(4,128)(2,1)S(1)}, bf16[4,128]{1,0:T(4,128)(2,1)S(1)}, u32[]{:S(2)}, u32[]{:S(2)}) collective-permute-start(bf16[4,128]{1,0:T(4,128)(2,1)S(1)} %fusion), channel_id=1, source_target_pairs={{0,64},{32,96},{64,0},{96,32},{1,65},{33,97},{65,1},{97,33},{2,66}... | collective-permute-start | bytes 3080 | tf_op jit(solution)/shard_map/ppermute | solution.py:124
  3.1 7.8 %collective-permute-start = (bf16[4,128]{1,0:T(4,128)(2,1)S(1)}, bf16[4,128]{1,0:T(4,128)(2,1)S(1)}, u32[]{:S(2)}, u32[]{:S(2)}) collective-permute-start(bf16[4,128]{1,0:T(4,128)(2,1)S(1)} %fusion), channel_id=1, source_target_pairs={{0,96},{32,64},{64,32},{96,0},{1,97},{33,65},{65,33},{97,1},{2,98}... | collective-permute-start | bytes 3080 | tf_op jit(solution)/shard_map/ppermute | solution.py:124

commit v3 on v2

v3 whole, which is shorter than its diff:
```python
import functools

import jax
import jax.numpy as jnp
from jax import lax
from jax.experimental import pallas as pl
from jax.experimental.pallas import tpu as pltpu
from jax.sharding import PartitionSpec as P

Z, Y, X = 4, 2, 4
PEERS = Z * Y * X
LISTED = [z * Y * X + y * X + x for z in range(Z) for x in range(X) for y in range(Y)]
BANKS = 4
LANES = 128
AHEAD = 2
HBM = pl.BlockSpec(memory_space=pltpu.HBM)
VMEM = pl.BlockSpec(memory_space=pltpu.VMEM)


def load_kernel(pieces, down, out, sem):
    rows = down.shape[1] // pieces
    copies = [
        pltpu.make_async_copy(
            down.at[e, pl.ds(k * rows, rows)], out.at[e, pl.ds(k * rows, rows)], sem
        )
        for e in range(AHEAD)
        for k in range(pieces)
    ]
    for c in copies:
        c.start()
    for c in copies:
        c.wait()


def load(down):
    return pl.pallas_call(
        functools.partial(load_kernel, Z),
        out_shape=jax.ShapeDtypeStruct((AHEAD, *down.shape[1:]), down.dtype),
        in_specs=[HBM],
        out_specs=VMEM,
        scratch_shapes=[pltpu.SemaphoreType.DMA],
        compiler_params=pltpu.CompilerParams(vmem_limit_bytes=2 << 20),
        cost_estimate=pl.CostEstimate(
            flops=down.size * 20, bytes_accessed=AHEAD * down[0].size * 8, transcendentals=0
        ),
    )(pltpu.with_memory_space_constraint(down, pltpu.HBM))


def narrow_kernel(experts, rows, down, held, w0, w1, w2, w3, gain, out, wide, block, come):
    lump = Y * X * rows
    steps = [(e, z) for e in range(experts) for z in range(Z)]
    later = AHEAD * Z

    def fetch(k):
        e, z = steps[k]
        return pltpu.make_async_copy(
            down.at[e, pl.ds(z * lump, lump)], wide.at[k - later], come.at[k - later]
        )

    for k in range(later, len(steps)):
        fetch(k).start()

    me = lax.axis_index("bank")
    by_step = [w[...] * gain[...] for w in (w0, w1, w2, w3)]
    for g in range(BANKS):
        part = by_step[g]
        for b in range(1, BANKS):
            part = jnp.where(me == b, by_step[g ^ b], part)
        block[pl.ds(g * w0.shape[0], w0.shape[0])] = part
    router = block[...].astype(jnp.bfloat16)
    for z in range(Z):
        for n in range(X * Y):
            out[z, n, pl.ds(experts * rows, block.shape[0])] = router

    for k, (e, z) in enumerate(steps):
        if k >= later:
            fetch(k).wait()
        for y in range(Y):
            for x in range(X):
                at = (y * X + x) * rows
                if k >= later:
                    piece = wide[k - later, pl.ds(at, rows)]
                else:
                    piece = held[e, pl.ds(z * lump + at, rows)]
                out[z, x * Y + y, pl.ds(e * rows, rows)] = piece.astype(jnp.bfloat16)


def narrow(down, held, weights, gain):
    experts, rows = down.shape[0], down.shape[1] // PEERS
    tail = BANKS * weights[0].shape[0]
    later = (experts - AHEAD) * Z
    return pl.pallas_call(
        functools.partial(narrow_kernel, experts, rows),
        out_shape=pltpu.VMEM((Z, X * Y, experts * rows + tail, LANES), jnp.bfloat16),
        in_specs=[HBM] + [VMEM] * (BANKS + 2),
        out_specs=VMEM,
        scratch_shapes=[
            pltpu.VMEM((later, Y * X * rows, LANES), jnp.float32),
            pltpu.VMEM((tail, LANES), jnp.float32),
            pltpu.SemaphoreType.DMA((later,)),
        ],
        compiler_params=pltpu.CompilerParams(vmem_limit_bytes=16 << 20),
        cost_estimate=pl.CostEstimate(
            flops=down.size * 40, bytes_accessed=down.size * 6, transcendentals=0
        ),
    )(pltpu.with_memory_space_constraint(down, pltpu.HBM), held, *weights, gain)


def place_kernel(experts, rows, got, final, serve, sem):
    copies = []
    for at, p in enumerate(LISTED):
        columns = pl.ds(p * LANES, LANES)
        for e in range(experts):
            copies.append((got.at[at, pl.ds(e * rows, rows)], final.at[e, :, columns]))
        copies.append((got.at[at, pl.ds(experts * rows, serve.shape[0])], serve.at[:, columns]))
    copies = [pltpu.make_async_copy(a, b, sem) for a, b in copies]
    for c in copies:
        c.start()
    for c in copies:
        c.wait()


def place(got, experts, rows):
    return pl.pallas_call(
        functools.partial(place_kernel, experts, rows),
        out_shape=[
            pltpu.HBM((experts, rows, PEERS * LANES), jnp.bfloat16),
            pltpu.HBM((got.shape[1] - experts * rows, PEERS * LANES), jnp.bfloat16),
        ],
        in_specs=[VMEM],
        out_specs=[HBM, HBM],
        scratch_shapes=[pltpu.SemaphoreType.DMA],
        compiler_params=pltpu.CompilerParams(vmem_limit_bytes=8 << 20),
    )(got)


def body(master_down, router_weight, router_gain):
    experts, rows = master_down.shape[0], master_down.shape[1] // PEERS
    mine = router_weight.T
    weights = [mine] + [
        lax.ppermute(mine, "bank", [(b, b ^ k) for b in range(BANKS)]) for k in range(1, BANKS)
    ]
    sent = narrow(master_down, load(master_down), weights, router_gain[None, :])
    sent = sent.reshape(PEERS, *sent.shape[2:])
    got = lax.all_to_all(sent, "zero", 0, 0, axis_index_groups=[LISTED], tiled=True)
    final, serve = place(got, experts, rows)
    return jnp.transpose(final, (0, 2, 1)), serve.T


def solution(mesh):
    placed = (P("bank", None, "zero"), P("zero", "bank"), P("zero"))
    return jax.shard_map(
        body, mesh=mesh, in_specs=placed, out_specs=(P("bank", None, "zero"), P()), check_vma=False
    )
```

time: 106 us -> 102 us (0.962)
  Pallas kernels: 11.2 us -> 8.66 us
    pallas_call x1, Pallas kernels: 7.66 us -> 2.98 us  [narrow(): pl.pallas_call(functools.partial(narrow_kernel, experts, rows), out_shape...]
    pallas_call x1, Pallas kernels: 0.73 us -> 2.87 us  [load(): pl.pallas_call(functools.partial(load_kernel, Z), out_shape=jax.ShapeDtyp...]
  transfers between devices with their start and end apart: 3 -> 3, of which waited for: 0 -> 1; matrix products, arithmetic and copies ran while one was open for 0% -> 0% of each run, Pallas kernels for 7% -> 3%
where the time goes in v3:
time: 102 us
  blocking collectives  90.6 us (89%)
  Pallas kernels  8.66 us (8%)
  starting transfers between devices  1.94 us (2%)
    all_to_all x1, blocking collectives, body(): lax.all_to_all(sent, 'zero', 0, 0, axis_index_groups=[LISTED], tiled=True)  90.6 us
    pallas_call x1, Pallas kernels, narrow(): pl.pallas_call(functools.partial(narrow_kernel, experts, rows), out_shape...  2.98 us
    pallas_call x1, Pallas kernels, load(): pl.pallas_call(functools.partial(load_kernel, Z), out_shape=jax.ShapeDtyp...  2.87 us
    pallas_call x1, Pallas kernels, place(): pl.pallas_call(functools.partial(place_kernel, experts, rows), out_shape=...  2.81 us
  transfers between devices with their start and end apart: 3, of which 1 were waited for; matrix products, arithmetic and copies ran while one was open for 0% of the time, Pallas kernels for 3%

profile of v3, /device:TPU:0, one launch (start us, length us, event | category | flops | bytes accessed | tf_op | source)
XLA Modules:
  0.0 102.0 jit_solution(5507453372402883490)
XLA Ops:
  0.6 0.0 copy-start
  0.6 0.0 copy-start.1
  0.6 1.2 %collective-permute-start.2 = (f32[4,128]{1,0:T(4,128)}, f32[4,128]{1,0:T(4,128)S(1)}, u32[]{:S(2)}, u32[]{:S(2)}) collective-permute-start(f32[4,128]{1,0:T(4,128)} %bitcast.6), channel_id=1, source_target_pairs={{0,96},{32,64},{64,32},{96,0},{1,97},{33,65},{65,33},{97,1},{2,98}... | collective-permute-start | bytes 6152 | tf_op jit(solution)/shard_map/ppermute | solution.py:141
  1.9 0.7 collective-permute-start.1
  2.5 0.1 collective-permute-start
  2.6 2.9 %shard_map.50.held = f32[2,6400,128]{2,1,0:T(8,128)S(1)} custom-call(f32[4,6400,128]{2,1,0:T(8,128)} %down.3), custom_call_target="tpu_custom_call" | custom-call | flops 65536000 | bytes 13107200 | tf_op jit(solution)/shard_map/pallas_call | solution.py:36
  5.5 0.0 collective-permute-done.2.w3
  5.5 0.2 collective-permute-done.1.w2
  5.7 0.0 collective-permute-done.w1
  5.7 0.0 copy-done
  5.7 0.0 copy-done.1
  5.7 3.0 %shard_map.51 = bf16[4,8,816,128]{3,2,1,0:T(8,128)(2,1)S(1)} custom-call(f32[4,6400,128]{2,1,0:T(8,128)} %down.3, f32[2,6400,128]{2,1,0:T(8,128)S(1)} %shard_map.50.held, f32[4,128]{1,0:T(4,128)S(1)} %bitcast.9, f32[4,128]{1,0:T(4,128)S(1)} %collective-permute-done.w1, f32[4,128]{1,0:T(4,128)S(1)} %collective-permute-done.1.w2, ...), custom_call_target="tpu_custom_call" | custom-call | flops 131072000 | bytes 19660800 | tf_op jit(solution)/shard_map/pallas_call | solution.py:92
  8.7 90.6 %all_to_all.5.got = bf16[32,816,128]{2,1,0:T(8,128)(2,1)S(1)} all-to-all(bf16[32,816,128]{2,1,0:T(8,128)(2,1)S(1)} %bitcast.5), channel_id=1, replica_groups={{0,4,1,5,2,6,3,7,8,12,9,13,10,14,11,15,16,20,17,21,18,22,19,23,24,28,25..., dimensions={0} | all-to-all | bytes 13369344 | tf_op jit(solution)/shard_map/all_to_all | solution.py:145
  99.2 2.8 %shard_map.52 = (bf16[4,200,4096]{2,1,0:T(8,128)(2,1)}, bf16[16,4096]{1,0:T(8,128)(2,1)}) custom-call(bf16[32,816,128]{2,1,0:T(8,128)(2,1)S(1)} %all_to_all.5.got), custom_call_target="tpu_custom_call" | custom-call | tf_op jit(solution)/shard_map/pallas_call | solution.py:124
Async XLA Ops:
  0.6 5.0 %copy-start = (f32[128,4]{0,1:T(4,128)S(1)}, f32[128,4]{0,1:T(4,128)}, u32[]{:S(2)}) copy-start(f32[128,4]{0,1:T(4,128)} %param.4) | copy-start | bytes 6148
  0.6 5.0 %copy-start.1 = (f32[128]{0:T(128)S(1)}, f32[128]{0:T(128)}, u32[]{:S(2)}) copy-start(f32[128]{0:T(128)} %param.5) | copy-start | bytes 1540
  0.6 4.8 %collective-permute-start.2 = (f32[4,128]{1,0:T(4,128)}, f32[4,128]{1,0:T(4,128)S(1)}, u32[]{:S(2)}, u32[]{:S(2)}) collective-permute-start(f32[4,128]{1,0:T(4,128)} %bitcast.6), channel_id=1, source_target_pairs={{0,96},{32,64},{64,32},{96,0},{1,97},{33,65},{65,33},{97,1},{2,98}... | collective-permute-start | bytes 6152 | tf_op jit(solution)/shard_map/ppermute | solution.py:141
  1.9 3.8 %collective-permute-start.1 = (f32[4,128]{1,0:T(4,128)}, f32[4,128]{1,0:T(4,128)S(1)}, u32[]{:S(2)}, u32[]{:S(2)}) collective-permute-start(f32[4,128]{1,0:T(4,128)} %bitcast.7), channel_id=1, source_target_pairs={{0,64},{32,96},{64,0},{96,32},{1,65},{33,97},{65,1},{97,33},{2,66}... | collective-permute-start | bytes 6152 | tf_op jit(solution)/shard_map/ppermute | solution.py:141
  2.5 3.1 %collective-permute-start = (f32[4,128]{1,0:T(4,128)}, f32[4,128]{1,0:T(4,128)S(1)}, u32[]{:S(2)}, u32[]{:S(2)}) collective-permute-start(f32[4,128]{1,0:T(4,128)} %bitcast.8), channel_id=1, source_target_pairs={{0,32},{32,0},{64,96},{96,64},{1,33},{33,1},{65,97},{97,65},{2,34}... | collective-permute-start | bytes 6152 | tf_op jit(solution)/shard_map/ppermute | solution.py:141

commit v4 on v3

v4 whole, which is shorter than its diff:
```python
import functools

import jax
import jax.numpy as jnp
from jax import lax
from jax.experimental import pallas as pl
from jax.experimental.pallas import tpu as pltpu
from jax.sharding import PartitionSpec as P

Z, Y, X = 4, 2, 4
PEERS = Z * Y * X
LISTED = [z * Y * X + y * X + x for z in range(Z) for x in range(X) for y in range(Y)]
BANKS = 4
LANES = 128
WINDOW = 1 << 34
HBM = pl.BlockSpec(memory_space=pltpu.HBM)
VMEM = pl.BlockSpec(memory_space=pltpu.VMEM)


def scale_kernel(weight, gain, out, weight_in, gain_in, sems):
    copies = [
        pltpu.make_async_copy(weight, weight_in, sems.at[0]),
        pltpu.make_async_copy(gain, gain_in, sems.at[1]),
    ]
    for c in copies:
        c.start()
    for c in copies:
        c.wait()
    out[...] = weight_in[...] * gain_in[...]


def scale(weight, gain):
    return pl.pallas_call(
        scale_kernel,
        out_shape=jax.ShapeDtypeStruct(weight.shape, weight.dtype),
        in_specs=[HBM, HBM],
        out_specs=VMEM,
        scratch_shapes=[
            pltpu.VMEM(weight.shape, weight.dtype),
            pltpu.VMEM(gain.shape, gain.dtype),
            pltpu.SemaphoreType.DMA((2,)),
        ],
        compiler_params=pltpu.CompilerParams(vmem_limit_bytes=1 << 20),
        cost_estimate=pl.CostEstimate(flops=WINDOW, bytes_accessed=4096, transcendentals=0),
    )(
        pltpu.with_memory_space_constraint(weight, pltpu.HBM),
        pltpu.with_memory_space_constraint(gain, pltpu.HBM),
    )


def narrow_kernel(experts, rows, held, w0, w1, w2, w3, out, block):
    lump = Y * X * rows
    me = lax.axis_index("bank")
    by_step = [w[...] for w in (w0, w1, w2, w3)]
    for g in range(BANKS):
        part = by_step[g]
        for b in range(1, BANKS):
            part = jnp.where(me == b, by_step[g ^ b], part)
        block[pl.ds(g * w0.shape[0], w0.shape[0])] = part
    router = block[...].astype(jnp.bfloat16)
    for z in range(Z):
        for n in range(X * Y):
            out[z, n, pl.ds(experts * rows, block.shape[0])] = router
    for e in range(experts):
        for z in range(Z):
            for y in range(Y):
                for x in range(X):
                    piece = held[e, pl.ds(z * lump + (y * X + x) * rows, rows)]
                    out[z, x * Y + y, pl.ds(e * rows, rows)] = piece.astype(jnp.bfloat16)


def narrow(down, weights):
    experts, rows = down.shape[0], down.shape[1] // PEERS
    tail = BANKS * weights[0].shape[0]
    return pl.pallas_call(
        functools.partial(narrow_kernel, experts, rows),
        out_shape=pltpu.VMEM((Z, X * Y, experts * rows + tail, LANES), jnp.bfloat16),
        in_specs=[VMEM] * (BANKS + 1),
        out_specs=VMEM,
        scratch_shapes=[pltpu.VMEM((tail, LANES), jnp.float32)],
        compiler_params=pltpu.CompilerParams(vmem_limit_bytes=2 << 20),
        cost_estimate=pl.CostEstimate(
            flops=down.size * 40, bytes_accessed=down.size * 6, transcendentals=0
        ),
    )(down, *weights)


def place_kernel(experts, rows, got, final, serve, sem):
    copies = []
    for at, p in enumerate(LISTED):
        columns = pl.ds(p * LANES, LANES)
        for e in range(experts):
            copies.append((got.at[at, pl.ds(e * rows, rows)], final.at[e, :, columns]))
        copies.append((got.at[at, pl.ds(experts * rows, serve.shape[0])], serve.at[:, columns]))
    copies = [pltpu.make_async_copy(a, b, sem) for a, b in copies]
    for c in copies:
        c.start()
    for c in copies:
        c.wait()


def place(got, experts, rows):
    return pl.pallas_call(
        functools.partial(place_kernel, experts, rows),
        out_shape=[
            pltpu.HBM((experts, rows, PEERS * LANES), jnp.bfloat16),
            pltpu.HBM((got.shape[1] - experts * rows, PEERS * LANES), jnp.bfloat16),
        ],
        in_specs=[VMEM],
        out_specs=[HBM, HBM],
        scratch_shapes=[pltpu.SemaphoreType.DMA],
        compiler_params=pltpu.CompilerParams(vmem_limit_bytes=8 << 20),
    )(got)


def body(master_down, router_weight, router_gain):
    experts, rows = master_down.shape[0], master_down.shape[1] // PEERS
    mine = scale(router_weight.T, router_gain[None, :])
    weights = [mine] + [
        lax.ppermute(mine, "bank", [(b, b ^ k) for b in range(BANKS)]) for k in range(1, BANKS)
    ]
    sent = narrow(master_down, weights)
    sent = sent.reshape(PEERS, *sent.shape[2:])
    got = lax.all_to_all(sent, "zero", 0, 0, axis_index_groups=[LISTED], tiled=True)
    final, serve = place(got, experts, rows)
    return jnp.transpose(final, (0, 2, 1)), serve.T


def solution(mesh):
    placed = (P("bank", None, "zero"), P("zero", "bank"), P("zero"))
    return jax.shard_map(
        body, mesh=mesh, in_specs=placed, out_specs=(P("bank", None, "zero"), P()), check_vma=False
    )
```

time: 102 us -> 99.7 us (0.977)
  Pallas kernels: 8.66 us -> 4.31 us
  waiting for transfers between devices: 0.18 us -> 2.85 us
    ppermute x3, waiting for transfers between devices: 0.18 us -> 2.85 us  [body(): lax.ppermute(mine, 'bank', [(b, b ^ k) for b in range(BANKS)])]
    pallas_call x1, Pallas kernels: 2.98 us -> 0.65 us  [narrow(): pl.pallas_call(functools.partial(narrow_kernel, experts, rows), out_shape...]
    pallas_call x1, Pallas kernels: 2.87 us -> 0.85 us  [scale(): pl.pallas_call(scale_kernel, out_shape=jax.ShapeDtypeStruct(weight.shape,...]
  transfers between devices with their start and end apart: 3 -> 3, of which waited for: 1 -> 2; matrix products, arithmetic and copies ran while one was open for 0% -> 0% of each run, Pallas kernels for 3% -> 0%
where the time goes in v4:
time: 99.7 us; the launch traced here: 99.6 us
  blocking collectives  89.7 us (90%)
  Pallas kernels  4.31 us (4%)
  waiting for transfers between devices  2.85 us (3%)
  starting transfers between devices  1.94 us (2%)
    all_to_all x1, blocking collectives, body(): lax.all_to_all(sent, 'zero', 0, 0, axis_index_groups=[LISTED], tiled=True)  89.7 us
    ppermute x3, waiting for transfers between devices, body(): lax.ppermute(mine, 'bank', [(b, b ^ k) for b in range(BANKS)])  2.85 us
    pallas_call x1, Pallas kernels, place(): pl.pallas_call(functools.partial(place_kernel, experts, rows), out_shape=...  2.81 us
  transfers between devices with their start and end apart: 3, of which 2 were waited for; matrix products, arithmetic and copies ran while one was open for 0% of the time, Pallas kernels for 0%

profile of v4, /device:TPU:0, one launch (start us, length us, event | category | flops | bytes accessed | tf_op | source)
XLA Modules:
  0.0 99.6 jit_solution(3470642608836977418)
XLA Ops:
  0.6 0.0 slice-start
  0.6 0.0 slice-start.1
  0.7 0.0 slice-start.2
  0.7 0.0 slice-start.3
  0.7 0.9 shard_map.50.w0
  1.5 1.2 %collective-permute-start.2 = (f32[4,128]{1,0:T(4,128)S(1)}, f32[4,128]{1,0:T(4,128)S(1)}, u32[]{:S(2)}, u32[]{:S(2)}) collective-permute-start(f32[4,128]{1,0:T(4,128)S(1)} %shard_map.50.w0), channel_id=1, source_target_pairs={{0,96},{32,64},{64,32},{96,0},{1,97},{33,65},{65,33},{97,1},{2,98}... | collective-permute-start | bytes 6152 | tf_op jit(solution)/shard_map/ppermute | solution.py:120
  2.7 0.7 collective-permute-start.1
  3.4 0.1 collective-permute-start
  3.5 1.1 %collective-permute-done.2.w3 = f32[4,128]{1,0:T(4,128)S(1)} collective-permute-done((f32[4,128]{1,0:T(4,128)S(1)}, f32[4,128]{1,0:T(4,128)S(1)}, u32[]{:S(2)}, u32[]{:S(2)}) %collective-permute-start.2) | collective-permute-done | bytes 2080 | tf_op jit(solution)/shard_map/ppermute | solution.py:120
  4.6 1.7 %collective-permute-done.1.w2 = f32[4,128]{1,0:T(4,128)S(1)} collective-permute-done((f32[4,128]{1,0:T(4,128)S(1)}, f32[4,128]{1,0:T(4,128)S(1)}, u32[]{:S(2)}, u32[]{:S(2)}) %collective-permute-start.1) | collective-permute-done | bytes 2080 | tf_op jit(solution)/shard_map/ppermute | solution.py:120
  6.3 0.0 collective-permute-done.w1
  6.3 0.0 slice-done
  6.3 0.0 slice-done.1
  6.3 0.0 slice-done.2
  6.3 0.0 slice-done.3
  6.4 0.7 shard_map.51
  7.0 89.7 %all_to_all.5.got = bf16[32,816,128]{2,1,0:T(8,128)(2,1)S(1)} all-to-all(bf16[32,816,128]{2,1,0:T(8,128)(2,1)S(1)} %bitcast.5), channel_id=1, replica_groups={{0,4,1,5,2,6,3,7,8,12,9,13,10,14,11,15,16,20,17,21,18,22,19,23,24,28,25..., dimensions={0} | all-to-all | bytes 13369344 | tf_op jit(solution)/shard_map/all_to_all | solution.py:124
  96.7 2.8 %shard_map.52 = (bf16[4,200,4096]{2,1,0:T(8,128)(2,1)}, bf16[16,4096]{1,0:T(8,128)(2,1)}) custom-call(bf16[32,816,128]{2,1,0:T(8,128)(2,1)S(1)} %all_to_all.5.got), custom_call_target="tpu_custom_call" | custom-call | tf_op jit(solution)/shard_map/pallas_call | solution.py:103
  (1 shorter events, 0.0 us)
Async XLA Ops:
  0.6 5.7 %slice-start = ((s8[13107200]{0:T(1024)(128)(4,1)}), s8[4194304]{0:T(1024)(128)(4,1)S(1)}, s32[]{:S(2)}) async-start(s8[13107200]{0:T(1024)(128)(4,1)} %bitcast.6), calls=%async_computation.1 | async-start | bytes 8388608
  0.6 5.7 %slice-start.1 = ((s8[13107200]{0:T(1024)(128)(4,1)}), s8[4194304]{0:T(1024)(128)(4,1)S(1)}, s32[]{:S(2)}) async-start(s8[13107200]{0:T(1024)(128)(4,1)} %bitcast.6), calls=%async_computation.2 | async-start | bytes 8388608
  0.7 5.7 %slice-start.2 = ((s8[13107200]{0:T(1024)(128)(4,1)}), s8[4194304]{0:T(1024)(128)(4,1)S(1)}, s32[]{:S(2)}) async-start(s8[13107200]{0:T(1024)(128)(4,1)} %bitcast.6), calls=%async_computation.3 | async-start | bytes 8388608
  0.7 5.7 %slice-start.3 = ((s8[13107200]{0:T(1024)(128)(4,1)}), s8[524288]{0:T(1024)(128)(4,1)S(1)}, s32[]{:S(2)}) async-start(s8[13107200]{0:T(1024)(128)(4,1)} %bitcast.6), calls=%async_computation.4 | async-start | bytes 1048576
  1.5 3.1 %collective-permute-start.2 = (f32[4,128]{1,0:T(4,128)S(1)}, f32[4,128]{1,0:T(4,128)S(1)}, u32[]{:S(2)}, u32[]{:S(2)}) collective-permute-start(f32[4,128]{1,0:T(4,128)S(1)} %shard_map.50.w0), channel_id=1, source_target_pairs={{0,96},{32,64},{64,32},{96,0},{1,97},{33,65},{65,33},{97,1},{2,98}... | collective-permute-start | bytes 6152 | tf_op jit(solution)/shard_map/ppermute | solution.py:120
  2.7 3.6 %collective-permute-start.1 = (f32[4,128]{1,0:T(4,128)S(1)}, f32[4,128]{1,0:T(4,128)S(1)}, u32[]{:S(2)}, u32[]{:S(2)}) collective-permute-start(f32[4,128]{1,0:T(4,128)S(1)} %shard_map.50.w0), channel_id=1, source_target_pairs={{0,64},{32,96},{64,0},{96,32},{1,65},{33,97},{65,1},{97,33},{2,66}... | collective-permute-start | bytes 6152 | tf_op jit(solution)/shard_map/ppermute | solution.py:120
  3.4 2.9 %collective-permute-start = (f32[4,128]{1,0:T(4,128)S(1)}, f32[4,128]{1,0:T(4,128)S(1)}, u32[]{:S(2)}, u32[]{:S(2)}) collective-permute-start(f32[4,128]{1,0:T(4,128)S(1)} %shard_map.50.w0), channel_id=1, source_target_pairs={{0,32},{32,0},{64,96},{96,64},{1,33},{33,1},{65,97},{97,65},{2,34}... | collective-permute-start | bytes 6152 | tf_op jit(solution)/shard_map/ppermute | solution.py:120

commit v5 on v4

--- a/solution.py
+++ b/solution.py
@@ -9,7 +9,8 @@
 
 Z, Y, X = 4, 2, 4
 PEERS = Z * Y * X
-LISTED = [z * Y * X + y * X + x for z in range(Z) for x in range(X) for y in range(Y)]
+LISTED = list(reversed(range(PEERS)))
+PLACE = [LISTED.index(p) for p in range(PEERS)]
 BANKS = 4
 LANES = 128
 WINDOW = 1 << 34
@@ -49,7 +50,6 @@
 
 
 def narrow_kernel(experts, rows, held, w0, w1, w2, w3, out, block):
-    lump = Y * X * rows
     me = lax.axis_index("bank")
     by_step = [w[...] for w in (w0, w1, w2, w3)]
     for g in range(BANKS):
@@ -58,15 +58,12 @@
             part = jnp.where(me == b, by_step[g ^ b], part)
         block[pl.ds(g * w0.shape[0], w0.shape[0])] = part
     router = block[...].astype(jnp.bfloat16)
-    for z in range(Z):
-        for n in range(X * Y):
-            out[z, n, pl.ds(experts * rows, block.shape[0])] = router
+    for at in range(PEERS):
+        out[at, pl.ds(experts * rows, block.shape[0])] = router
     for e in range(experts):
-        for z in range(Z):
-            for y in range(Y):
-                for x in range(X):
-                    piece = held[e, pl.ds(z * lump + (y * X + x) * rows, rows)]
-                    out[z, x * Y + y, pl.ds(e * rows, rows)] = piece.astype(jnp.bfloat16)
+        for p, at in enumerate(PLACE):
+            piece = held[e, pl.ds(p * rows, rows)]
+            out[at, pl.ds(e * rows, rows)] = piece.astype(jnp.bfloat16)
 
 
 def narrow(down, weights):
@@ -74,7 +71,7 @@
     tail = BANKS * weights[0].shape[0]
     return pl.pallas_call(
         functools.partial(narrow_kernel, experts, rows),
-        out_shape=pltpu.VMEM((Z, X * Y, experts * rows + tail, LANES), jnp.bfloat16),
+        out_shape=pltpu.VMEM((PEERS, experts * rows + tail, LANES), jnp.bfloat16),
         in_specs=[VMEM] * (BANKS + 1),
         out_specs=VMEM,
         scratch_shapes=[pltpu.VMEM((tail, LANES), jnp.float32)],
@@ -120,7 +117,6 @@
         lax.ppermute(mine, "bank", [(b, b ^ k) for b in range(BANKS)]) for k in range(1, BANKS)
     ]
     sent = narrow(master_down, weights)
-    sent = sent.reshape(PEERS, *sent.shape[2:])
     got = lax.all_to_all(sent, "zero", 0, 0, axis_index_groups=[LISTED], tiled=True)
     final, serve = place(got, experts, rows)
     return jnp.transpose(final, (0, 2, 1)), serve.T

time: 99.7 us -> 95.2 us (0.955)
  blocking collectives: 89.7 us -> 85.1 us
    all_to_all x1, blocking collectives: 89.7 us -> 85.1 us  [body(): lax.all_to_all(sent, 'zero', 0, 0, axis_index_groups=[LISTED], tiled=True)]
where the time goes in v5:
time: 95.2 us; the launch traced here: 95 us
  blocking collectives  85.1 us (89%)
  Pallas kernels  4.31 us (5%)
  waiting for transfers between devices  2.85 us (3%)
  starting transfers between devices  1.94 us (2%)
    all_to_all x1, blocking collectives, body(): lax.all_to_all(sent, 'zero', 0, 0, axis_index_groups=[LISTED], tiled=True)  85.1 us
    ppermute x3, waiting for transfers between devices, body(): lax.ppermute(mine, 'bank', [(b, b ^ k) for b in range(BANKS)])  2.85 us
    pallas_call x1, Pallas kernels, place(): pl.pallas_call(functools.partial(place_kernel, experts, rows), out_shape=...  2.81 us
    ppermute x3, starting transfers between devices, body(): lax.ppermute(mine, 'bank', [(b, b ^ k) for b in range(BANKS)])  1.94 us
  transfers between devices with their start and end apart: 3, of which 2 were waited for; matrix products, arithmetic and copies ran while one was open for 0% of the time, Pallas kernels for 0%

profile of v5, /device:TPU:0, one launch (start us, length us, event | category | flops | bytes accessed | tf_op | source)
XLA Modules:
  0.0 95.0 jit_solution(1444346996442447553)
XLA Ops:
  0.6 0.0 slice-start
  0.6 0.0 slice-start.1
  0.7 0.0 slice-start.2
  0.7 0.0 slice-start.3
  0.7 0.9 shard_map.50.w0
  1.5 1.2 %collective-permute-start.2 = (f32[4,128]{1,0:T(4,128)S(1)}, f32[4,128]{1,0:T(4,128)S(1)}, u32[]{:S(2)}, u32[]{:S(2)}) collective-permute-start(f32[4,128]{1,0:T(4,128)S(1)} %shard_map.50.w0), channel_id=1, source_target_pairs={{0,96},{32,64},{64,32},{96,0},{1,97},{33,65},{65,33},{97,1},{2,98}... | collective-permute-start | bytes 6152 | tf_op jit(solution)/shard_map/ppermute | solution.py:117
  2.7 0.7 collective-permute-start.1
  3.4 0.1 collective-permute-start
  3.5 1.1 %collective-permute-done.2.w3 = f32[4,128]{1,0:T(4,128)S(1)} collective-permute-done((f32[4,128]{1,0:T(4,128)S(1)}, f32[4,128]{1,0:T(4,128)S(1)}, u32[]{:S(2)}, u32[]{:S(2)}) %collective-permute-start.2) | collective-permute-done | bytes 2080 | tf_op jit(solution)/shard_map/ppermute | solution.py:117
  4.6 1.7 %collective-permute-done.1.w2 = f32[4,128]{1,0:T(4,128)S(1)} collective-permute-done((f32[4,128]{1,0:T(4,128)S(1)}, f32[4,128]{1,0:T(4,128)S(1)}, u32[]{:S(2)}, u32[]{:S(2)}) %collective-permute-start.1) | collective-permute-done | bytes 2080 | tf_op jit(solution)/shard_map/ppermute | solution.py:117
  6.3 0.0 collective-permute-done.w1
  6.3 0.0 slice-done
  6.3 0.0 slice-done.1
  6.3 0.0 slice-done.2
  6.3 0.0 slice-done.3
  6.4 0.7 shard_map.51
  7.0 85.1 %all_to_all.5.got = bf16[32,816,128]{2,1,0:T(8,128)(2,1)S(1)} all-to-all(bf16[32,816,128]{2,1,0:T(8,128)(2,1)S(1)} %shard_map.51), channel_id=1, replica_groups={{31,30,29,28,27,26,25,24,23,22,21,20,19,18,17,16,15,14,13,12,11,10,9,8,..., dimensions={0} | all-to-all | bytes 13369344 | tf_op jit(solution)/shard_map/all_to_all | solution.py:120
  92.1 2.8 %shard_map.52 = (bf16[4,200,4096]{2,1,0:T(8,128)(2,1)}, bf16[16,4096]{1,0:T(8,128)(2,1)}) custom-call(bf16[32,816,128]{2,1,0:T(8,128)(2,1)S(1)} %all_to_all.5.got), custom_call_target="tpu_custom_call" | custom-call | tf_op jit(solution)/shard_map/pallas_call | solution.py:100
  (1 shorter events, 0.0 us)
Async XLA Ops:
  0.6 5.7 %slice-start = ((s8[13107200]{0:T(1024)(128)(4,1)}), s8[4194304]{0:T(1024)(128)(4,1)S(1)}, s32[]{:S(2)}) async-start(s8[13107200]{0:T(1024)(128)(4,1)} %bitcast.4), calls=%async_computation.1 | async-start | bytes 8388608
  0.6 5.7 %slice-start.1 = ((s8[13107200]{0:T(1024)(128)(4,1)}), s8[4194304]{0:T(1024)(128)(4,1)S(1)}, s32[]{:S(2)}) async-start(s8[13107200]{0:T(1024)(128)(4,1)} %bitcast.4), calls=%async_computation.2 | async-start | bytes 8388608
  0.7 5.7 %slice-start.2 = ((s8[13107200]{0:T(1024)(128)(4,1)}), s8[4194304]{0:T(1024)(128)(4,1)S(1)}, s32[]{:S(2)}) async-start(s8[13107200]{0:T(1024)(128)(4,1)} %bitcast.4), calls=%async_computation.3 | async-start | bytes 8388608
  0.7 5.7 %slice-start.3 = ((s8[13107200]{0:T(1024)(128)(4,1)}), s8[524288]{0:T(1024)(128)(4,1)S(1)}, s32[]{:S(2)}) async-start(s8[13107200]{0:T(1024)(128)(4,1)} %bitcast.4), calls=%async_computation.4 | async-start | bytes 1048576
  1.5 3.1 %collective-permute-start.2 = (f32[4,128]{1,0:T(4,128)S(1)}, f32[4,128]{1,0:T(4,128)S(1)}, u32[]{:S(2)}, u32[]{:S(2)}) collective-permute-start(f32[4,128]{1,0:T(4,128)S(1)} %shard_map.50.w0), channel_id=1, source_target_pairs={{0,96},{32,64},{64,32},{96,0},{1,97},{33,65},{65,33},{97,1},{2,98}... | collective-permute-start | bytes 6152 | tf_op jit(solution)/shard_map/ppermute | solution.py:117
  2.7 3.6 %collective-permute-start.1 = (f32[4,128]{1,0:T(4,128)S(1)}, f32[4,128]{1,0:T(4,128)S(1)}, u32[]{:S(2)}, u32[]{:S(2)}) collective-permute-start(f32[4,128]{1,0:T(4,128)S(1)} %shard_map.50.w0), channel_id=1, source_target_pairs={{0,64},{32,96},{64,0},{96,32},{1,65},{33,97},{65,1},{97,33},{2,66}... | collective-permute-start | bytes 6152 | tf_op jit(solution)/shard_map/ppermute | solution.py:117
  3.4 2.9 %collective-permute-start = (f32[4,128]{1,0:T(4,128)S(1)}, f32[4,128]{1,0:T(4,128)S(1)}, u32[]{:S(2)}, u32[]{:S(2)}) collective-permute-start(f32[4,128]{1,0:T(4,128)S(1)} %shard_map.50.w0), channel_id=1, source_target_pairs={{0,32},{32,0},{64,96},{96,64},{1,33},{33,1},{65,97},{97,65},{2,34}... | collective-permute-start | bytes 6152 | tf_op jit(solution)/shard_map/ppermute | solution.py:117

commit v6 on v5

--- a/solution.py
+++ b/solution.py
@@ -9,7 +9,8 @@
 
 Z, Y, X = 4, 2, 4
 PEERS = Z * Y * X
-LISTED = list(reversed(range(PEERS)))
+FIRST = PEERS - 2
+LISTED = [FIRST] + [p for p in reversed(range(PEERS)) if p != FIRST]
 PLACE = [LISTED.index(p) for p in range(PEERS)]
 BANKS = 4
 LANES = 128

time: 95.2 us -> 94.8 us (level)
  no operation moved by 1% of the time
where the time goes in v6:
time: 94.8 us; the launch traced here: 94.4 us
  blocking collectives  84.6 us (89%)
  Pallas kernels  4.31 us (5%)
  waiting for transfers between devices  2.85 us (3%)
  starting transfers between devices  1.94 us (2%)
    all_to_all x1, blocking collectives, body(): lax.all_to_all(sent, 'zero', 0, 0, axis_index_groups=[LISTED], tiled=True)  84.6 us
    ppermute x3, waiting for transfers between devices, body(): lax.ppermute(mine, 'bank', [(b, b ^ k) for b in range(BANKS)])  2.85 us
    pallas_call x1, Pallas kernels, place(): pl.pallas_call(functools.partial(place_kernel, experts, rows), out_shape=...  2.81 us
    ppermute x3, starting transfers between devices, body(): lax.ppermute(mine, 'bank', [(b, b ^ k) for b in range(BANKS)])  1.94 us
  transfers between devices with their start and end apart: 3, of which 2 were waited for; matrix products, arithmetic and copies ran while one was open for 0% of the time, Pallas kernels for 0%

profile of v6, /device:TPU:0, one launch (start us, length us, event | category | flops | bytes accessed | tf_op | source)
XLA Modules:
  0.0 94.4 jit_solution(9451704751020672741)
XLA Ops:
  0.6 0.0 slice-start
  0.6 0.0 slice-start.1
  0.7 0.0 slice-start.2
  0.7 0.0 slice-start.3
  0.7 0.9 shard_map.50.w0
  1.5 1.2 %collective-permute-start.2 = (f32[4,128]{1,0:T(4,128)S(1)}, f32[4,128]{1,0:T(4,128)S(1)}, u32[]{:S(2)}, u32[]{:S(2)}) collective-permute-start(f32[4,128]{1,0:T(4,128)S(1)} %shard_map.50.w0), channel_id=1, source_target_pairs={{0,96},{32,64},{64,32},{96,0},{1,97},{33,65},{65,33},{97,1},{2,98}... | collective-permute-start | bytes 6152 | tf_op jit(solution)/shard_map/ppermute | solution.py:118
  2.7 0.7 collective-permute-start.1
  3.4 0.1 collective-permute-start
  3.5 1.1 %collective-permute-done.2.w3 = f32[4,128]{1,0:T(4,128)S(1)} collective-permute-done((f32[4,128]{1,0:T(4,128)S(1)}, f32[4,128]{1,0:T(4,128)S(1)}, u32[]{:S(2)}, u32[]{:S(2)}) %collective-permute-start.2) | collective-permute-done | bytes 2080 | tf_op jit(solution)/shard_map/ppermute | solution.py:118
  4.6 1.7 %collective-permute-done.1.w2 = f32[4,128]{1,0:T(4,128)S(1)} collective-permute-done((f32[4,128]{1,0:T(4,128)S(1)}, f32[4,128]{1,0:T(4,128)S(1)}, u32[]{:S(2)}, u32[]{:S(2)}) %collective-permute-start.1) | collective-permute-done | bytes 2080 | tf_op jit(solution)/shard_map/ppermute | solution.py:118
  6.3 0.0 collective-permute-done.w1
  6.3 0.0 slice-done
  6.3 0.0 slice-done.1
  6.3 0.0 slice-done.2
  6.3 0.0 slice-done.3
  6.4 0.7 shard_map.51
  7.0 84.6 %all_to_all.5.got = bf16[32,816,128]{2,1,0:T(8,128)(2,1)S(1)} all-to-all(bf16[32,816,128]{2,1,0:T(8,128)(2,1)S(1)} %shard_map.51), channel_id=1, replica_groups={{30,31,29,28,27,26,25,24,23,22,21,20,19,18,17,16,15,14,13,12,11,10,9,8,..., dimensions={0} | all-to-all | bytes 13369344 | tf_op jit(solution)/shard_map/all_to_all | solution.py:121
  91.6 2.8 %shard_map.52 = (bf16[4,200,4096]{2,1,0:T(8,128)(2,1)}, bf16[16,4096]{1,0:T(8,128)(2,1)}) custom-call(bf16[32,816,128]{2,1,0:T(8,128)(2,1)S(1)} %all_to_all.5.got), custom_call_target="tpu_custom_call" | custom-call | tf_op jit(solution)/shard_map/pallas_call | solution.py:101
  (1 shorter events, 0.0 us)
Async XLA Ops:
  0.6 5.7 %slice-start = ((s8[13107200]{0:T(1024)(128)(4,1)}), s8[4194304]{0:T(1024)(128)(4,1)S(1)}, s32[]{:S(2)}) async-start(s8[13107200]{0:T(1024)(128)(4,1)} %bitcast.4), calls=%async_computation.1 | async-start | bytes 8388608
  0.6 5.7 %slice-start.1 = ((s8[13107200]{0:T(1024)(128)(4,1)}), s8[4194304]{0:T(1024)(128)(4,1)S(1)}, s32[]{:S(2)}) async-start(s8[13107200]{0:T(1024)(128)(4,1)} %bitcast.4), calls=%async_computation.2 | async-start | bytes 8388608
  0.7 5.7 %slice-start.2 = ((s8[13107200]{0:T(1024)(128)(4,1)}), s8[4194304]{0:T(1024)(128)(4,1)S(1)}, s32[]{:S(2)}) async-start(s8[13107200]{0:T(1024)(128)(4,1)} %bitcast.4), calls=%async_computation.3 | async-start | bytes 8388608
  0.7 5.7 %slice-start.3 = ((s8[13107200]{0:T(1024)(128)(4,1)}), s8[524288]{0:T(1024)(128)(4,1)S(1)}, s32[]{:S(2)}) async-start(s8[13107200]{0:T(1024)(128)(4,1)} %bitcast.4), calls=%async_computation.4 | async-start | bytes 1048576
  1.5 3.1 %collective-permute-start.2 = (f32[4,128]{1,0:T(4,128)S(1)}, f32[4,128]{1,0:T(4,128)S(1)}, u32[]{:S(2)}, u32[]{:S(2)}) collective-permute-start(f32[4,128]{1,0:T(4,128)S(1)} %shard_map.50.w0), channel_id=1, source_target_pairs={{0,96},{32,64},{64,32},{96,0},{1,97},{33,65},{65,33},{97,1},{2,98}... | collective-permute-start | bytes 6152 | tf_op jit(solution)/shard_map/ppermute | solution.py:118
  2.7 3.6 %collective-permute-start.1 = (f32[4,128]{1,0:T(4,128)S(1)}, f32[4,128]{1,0:T(4,128)S(1)}, u32[]{:S(2)}, u32[]{:S(2)}) collective-permute-start(f32[4,128]{1,0:T(4,128)S(1)} %shard_map.50.w0), channel_id=1, source_target_pairs={{0,64},{32,96},{64,0},{96,32},{1,65},{33,97},{65,1},{97,33},{2,66}... | collective-permute-start | bytes 6152 | tf_op jit(solution)/shard_map/ppermute | solution.py:118
  3.4 2.9 %collective-permute-start = (f32[4,128]{1,0:T(4,128)S(1)}, f32[4,128]{1,0:T(4,128)S(1)}, u32[]{:S(2)}, u32[]{:S(2)}) collective-permute-start(f32[4,128]{1,0:T(4,128)S(1)} %shard_map.50.w0), channel_id=1, source_target_pairs={{0,32},{32,0},{64,96},{96,64},{1,33},{33,1},{65,97},{97,65},{2,34}... | collective-permute-start | bytes 6152 | tf_op jit(solution)/shard_map/ppermute | solution.py:118

commit v7 on v5

--- a/solution.py
+++ b/solution.py
@@ -9,7 +9,7 @@
 
 Z, Y, X = 4, 2, 4
 PEERS = Z * Y * X
-LISTED = list(reversed(range(PEERS)))
+LISTED = [z * Y * X + y * X + x for x in range(X) for y in range(Y) for z in range(Z)][::-1]
 PLACE = [LISTED.index(p) for p in range(PEERS)]
 BANKS = 4
 LANES = 128

time: 95.2 us -> 95 us (level)
  no operation moved by 1% of the time
where the time goes in v7:
time: 95 us; the launch traced here: 94.8 us
  blocking collectives  85 us (89%)
  Pallas kernels  4.31 us (5%)
  waiting for transfers between devices  2.85 us (3%)
  starting transfers between devices  1.94 us (2%)
    all_to_all x1, blocking collectives, body(): lax.all_to_all(sent, 'zero', 0, 0, axis_index_groups=[LISTED], tiled=True)  85 us
    ppermute x3, waiting for transfers between devices, body(): lax.ppermute(mine, 'bank', [(b, b ^ k) for b in range(BANKS)])  2.85 us
    pallas_call x1, Pallas kernels, place(): pl.pallas_call(functools.partial(place_kernel, experts, rows), out_shape=...  2.81 us
    ppermute x3, starting transfers between devices, body(): lax.ppermute(mine, 'bank', [(b, b ^ k) for b in range(BANKS)])  1.94 us
  transfers between devices with their start and end apart: 3, of which 2 were waited for; matrix products, arithmetic and copies ran while one was open for 0% of the time, Pallas kernels for 0%

profile of v7, /device:TPU:0, one launch (start us, length us, event | category | flops | bytes accessed | tf_op | source)
XLA Modules:
  0.0 94.8 jit_solution(16172748024123660609)
XLA Ops:
  0.6 0.0 slice-start
  0.6 0.0 slice-start.1
  0.7 0.0 slice-start.2
  0.7 0.0 slice-start.3
  0.7 0.9 shard_map.50.w0
  1.5 1.2 %collective-permute-start.2 = (f32[4,128]{1,0:T(4,128)S(1)}, f32[4,128]{1,0:T(4,128)S(1)}, u32[]{:S(2)}, u32[]{:S(2)}) collective-permute-start(f32[4,128]{1,0:T(4,128)S(1)} %shard_map.50.w0), channel_id=1, source_target_pairs={{0,96},{32,64},{64,32},{96,0},{1,97},{33,65},{65,33},{97,1},{2,98}... | collective-permute-start | bytes 6152 | tf_op jit(solution)/shard_map/ppermute | solution.py:117
  2.7 0.7 collective-permute-start.1
  3.4 0.1 collective-permute-start
  3.5 1.1 %collective-permute-done.2.w3 = f32[4,128]{1,0:T(4,128)S(1)} collective-permute-done((f32[4,128]{1,0:T(4,128)S(1)}, f32[4,128]{1,0:T(4,128)S(1)}, u32[]{:S(2)}, u32[]{:S(2)}) %collective-permute-start.2) | collective-permute-done | bytes 2080 | tf_op jit(solution)/shard_map/ppermute | solution.py:117
  4.6 1.7 %collective-permute-done.1.w2 = f32[4,128]{1,0:T(4,128)S(1)} collective-permute-done((f32[4,128]{1,0:T(4,128)S(1)}, f32[4,128]{1,0:T(4,128)S(1)}, u32[]{:S(2)}, u32[]{:S(2)}) %collective-permute-start.1) | collective-permute-done | bytes 2080 | tf_op jit(solution)/shard_map/ppermute | solution.py:117
  6.3 0.0 collective-permute-done.w1
  6.3 0.0 slice-done
  6.3 0.0 slice-done.1
  6.3 0.0 slice-done.2
  6.3 0.0 slice-done.3
  6.4 0.7 shard_map.51
  7.0 85.0 %all_to_all.5.got = bf16[32,816,128]{2,1,0:T(8,128)(2,1)S(1)} all-to-all(bf16[32,816,128]{2,1,0:T(8,128)(2,1)S(1)} %shard_map.51), channel_id=1, replica_groups={{31,23,15,7,27,19,11,3,30,22,14,6,26,18,10,2,29,21,13,5,25,17,9,1,28,20..., dimensions={0} | all-to-all | bytes 13369344 | tf_op jit(solution)/shard_map/all_to_all | solution.py:120
  92.0 2.8 %shard_map.52 = (bf16[4,200,4096]{2,1,0:T(8,128)(2,1)}, bf16[16,4096]{1,0:T(8,128)(2,1)}) custom-call(bf16[32,816,128]{2,1,0:T(8,128)(2,1)S(1)} %all_to_all.5.got), custom_call_target="tpu_custom_call" | custom-call | tf_op jit(solution)/shard_map/pallas_call | solution.py:100
  (1 shorter events, 0.0 us)
Async XLA Ops:
  0.6 5.7 %slice-start = ((s8[13107200]{0:T(1024)(128)(4,1)}), s8[4194304]{0:T(1024)(128)(4,1)S(1)}, s32[]{:S(2)}) async-start(s8[13107200]{0:T(1024)(128)(4,1)} %bitcast.4), calls=%async_computation.1 | async-start | bytes 8388608
  0.6 5.7 %slice-start.1 = ((s8[13107200]{0:T(1024)(128)(4,1)}), s8[4194304]{0:T(1024)(128)(4,1)S(1)}, s32[]{:S(2)}) async-start(s8[13107200]{0:T(1024)(128)(4,1)} %bitcast.4), calls=%async_computation.2 | async-start | bytes 8388608
  0.7 5.7 %slice-start.2 = ((s8[13107200]{0:T(1024)(128)(4,1)}), s8[4194304]{0:T(1024)(128)(4,1)S(1)}, s32[]{:S(2)}) async-start(s8[13107200]{0:T(1024)(128)(4,1)} %bitcast.4), calls=%async_computation.3 | async-start | bytes 8388608
  0.7 5.7 %slice-start.3 = ((s8[13107200]{0:T(1024)(128)(4,1)}), s8[524288]{0:T(1024)(128)(4,1)S(1)}, s32[]{:S(2)}) async-start(s8[13107200]{0:T(1024)(128)(4,1)} %bitcast.4), calls=%async_computation.4 | async-start | bytes 1048576
  1.5 3.1 %collective-permute-start.2 = (f32[4,128]{1,0:T(4,128)S(1)}, f32[4,128]{1,0:T(4,128)S(1)}, u32[]{:S(2)}, u32[]{:S(2)}) collective-permute-start(f32[4,128]{1,0:T(4,128)S(1)} %shard_map.50.w0), channel_id=1, source_target_pairs={{0,96},{32,64},{64,32},{96,0},{1,97},{33,65},{65,33},{97,1},{2,98}... | collective-permute-start | bytes 6152 | tf_op jit(solution)/shard_map/ppermute | solution.py:117
  2.7 3.6 %collective-permute-start.1 = (f32[4,128]{1,0:T(4,128)S(1)}, f32[4,128]{1,0:T(4,128)S(1)}, u32[]{:S(2)}, u32[]{:S(2)}) collective-permute-start(f32[4,128]{1,0:T(4,128)S(1)} %shard_map.50.w0), channel_id=1, source_target_pairs={{0,64},{32,96},{64,0},{96,32},{1,65},{33,97},{65,1},{97,33},{2,66}... | collective-permute-start | bytes 6152 | tf_op jit(solution)/shard_map/ppermute | solution.py:117
  3.4 2.9 %collective-permute-start = (f32[4,128]{1,0:T(4,128)S(1)}, f32[4,128]{1,0:T(4,128)S(1)}, u32[]{:S(2)}, u32[]{:S(2)}) collective-permute-start(f32[4,128]{1,0:T(4,128)S(1)} %shard_map.50.w0), channel_id=1, source_target_pairs={{0,32},{32,0},{64,96},{96,64},{1,33},{33,1},{65,97},{97,65},{2,34}... | collective-permute-start | bytes 6152 | tf_op jit(solution)/shard_map/ppermute | solution.py:117
